TPU v7x, 128 devices: a whole 4x4x4 slice. The times are simulated.
128 devices in a mesh: gx: 16 (over z, x), gy: 8 (over y, core).
Axes of the slice: x: 4, y: 4, z: 4, core: 2. Of those that a mesh axis runs over, the one named last changes fastest.
Arguments:
- pressure: float32 [10, 1024, 4096], P(None, 'gx', 'gy'), may hold values from -6 to 6
- pressure_old: float32 [10, 1024, 4096], P(None, 'gx', 'gy'), may hold values from -6 to 6
- conductivity: float32 [10, 1024, 4096], P(None, 'gx', 'gy'), may hold values from 0.1 to 1
- porosity: float32 [10, 1024, 4096], P(None, 'gx', 'gy'), may hold values from 2 to 8
- recharge: float32 [1024, 4096], P('gx', 'gy'), may hold values from -6 to 6
- active: int32 [1024, 4096], P('gx', 'gy'), may hold values from 0 to 1, as said below
Outputs:
- final_pressure: float32 [10, 1024, 4096], P(None, 'gx', 'gy')
- linear_residual: float32 [10, 1024, 4096], P(None, 'gx', 'gy')
Inputs may be any that keep to these rules, and one draw needn't show every extreme that they name: `active`: 1 marks a land column, 0 an ocean column.
All inputs are finite; a program needn't handle non-finite values.
Results may differ from a plain program's by a relative error of at most 0.0003.
Values sent between devices are 32-bit elements; how exact they have to be, the bound alone decides.
No kernel may reach another device: no remote copies, remote signals or barrier semaphores. Data moves between devices by JAX's collectives and lax.ppermute only.
A program may use at most 128 MiB of HBM per device.

v0:
```python
import jax
import jax.numpy as jnp
from jax import lax
from jax.sharding import Mesh
from jax.sharding import PartitionSpec as P

NEWTON = 2
GX_GY = ("gx_0", "gx_1", "gy_0", "gy_1")
GX = ("gx_0", "gx_1")
GY = ("gy_0", "gy_1")
residual_sat = 0.1
vertical_factor = 2.0
epsilon = 1e-06


def padded(value, sides, width):
    edges = {}
    for axis, dim in sides:
        size, length = (lax.axis_size(axis), value.shape[dim])
        up = [(i, (i + 1) % size) for i in range(size - 1)]
        last = lax.slice_in_dim(value, length - width, length, axis=dim)
        initial = lax.slice_in_dim(value, 0, width, axis=dim)
        edges[dim] = (
            lax.ppermute(last, axis, up),
            lax.ppermute(initial, axis, [(b, a) for a, b in up]),
        )
    done = []
    for _, dim in sides:
        low, high = edges[dim]
        around = [(width, width) if d in done else (0, 0) for d in range(value.ndim)]
        value = jnp.concatenate([jnp.pad(low, around), value, jnp.pad(high, around)], axis=dim)
        done.append(dim)
    return value


def by_axis(value, axes):
    for axis in axes:
        value = lax.psum(value, axis)
    return value


def interior(array):
    return array[:, 1:-1, 1:-1]


def saturation(values):
    return residual_sat + (1.0 - residual_sat) * jax.nn.sigmoid(values)


def sat_slope(values):
    sigma = jax.nn.sigmoid(values)
    return (1.0 - residual_sat) * sigma * (1.0 - sigma)


def face_pair(press_low, press_high, cond_low, cond_high, act_low, act_high, factor, gravity):
    transmit = 0.5 * factor * (cond_low + cond_high) * act_low * act_high
    sig_low = jax.nn.sigmoid(press_low)
    sig_high = jax.nn.sigmoid(press_high)
    mobility = 0.5 * (sig_low * sig_low + sig_high * sig_high)
    head_drop = press_low - press_high + gravity
    coef_low = transmit * (mobility + sig_low * sig_low * (1.0 - sig_low) * head_drop)
    coef_high = transmit * (sig_high * sig_high * (1.0 - sig_high) * head_drop - mobility)
    return (coef_low, coef_high, transmit * mobility * head_drop)


def coefficients(pressure, conduct, active):
    across_x = face_pair(
        pressure[:, :-1, 1:-1],
        pressure[:, 1:, 1:-1],
        conduct[:, :-1, 1:-1],
        conduct[:, 1:, 1:-1],
        active[:, :-1, 1:-1],
        active[:, 1:, 1:-1],
        1.0,
        0.0,
    )
    across_y = face_pair(
        pressure[:, 1:-1, :-1],
        pressure[:, 1:-1, 1:],
        conduct[:, 1:-1, :-1],
        conduct[:, 1:-1, 1:],
        active[:, 1:-1, :-1],
        active[:, 1:-1, 1:],
        1.0,
        0.0,
    )
    inner_p = interior(pressure)
    inner_k = interior(conduct)
    inner_a = interior(active)
    across_z = face_pair(
        inner_p[:-1],
        inner_p[1:],
        inner_k[:-1],
        inner_k[1:],
        inner_a[:-1],
        inner_a[1:],
        vertical_factor,
        -1.0,
    )
    return (across_x, across_y, across_z)


def outflow(flow_x, flow_y, flow_z):
    total = flow_x[:, 1:] - flow_x[:, :-1] + flow_y[:, :, 1:] - flow_y[:, :, :-1]
    zeros = jnp.zeros_like(flow_z[:1])
    return total + jnp.concatenate([flow_z, zeros], 0) - jnp.concatenate([zeros, flow_z], 0)


def jacobian_apply(vector, faces, diagonal, active):
    x_low, x_high, x_flow = faces[0]
    y_low, y_high, y_flow = faces[1]
    z_low, z_high, z_flow = faces[2]
    flow_x = x_low * vector[:, :-1, 1:-1] + x_high * vector[:, 1:, 1:-1]
    flow_y = y_low * vector[:, 1:-1, :-1] + y_high * vector[:, 1:-1, 1:]
    center = interior(vector)
    flow_z = z_low * center[:-1] + z_high * center[1:]
    return active * (diagonal * center + outflow(flow_x, flow_y, flow_z)) + (1.0 - active) * center


def newton_residual(pressure, faces, pressure_old, porosity, recharge, active):
    center = interior(pressure)
    storage = porosity * (saturation(center) - saturation(pressure_old))
    inflow = jnp.concatenate([jnp.zeros_like(center[:-1]), recharge[None]], 0)
    flows = outflow(faces[0][2], faces[1][2], faces[2][2])
    return active * (storage - inflow + flows) + (1.0 - active) * center


def least_squares(first_norm, entry_one, entry_two, entry_three, entry_four, entry_five):
    radius = jnp.sqrt(entry_one * entry_one + entry_two * entry_two)
    cosine = entry_one / radius
    sine = entry_two / radius
    top_right = cosine * entry_three + sine * entry_four
    lower = cosine * entry_four - sine * entry_three
    weight_two = -lower * sine * first_norm / (lower * lower + entry_five * entry_five)
    weight_one = (cosine * first_norm - top_right * weight_two) / radius
    return (weight_one, weight_two)


def body(pressure, pressure_old, conductivity, porosity, recharge, active):
    layers = pressure.shape[0]
    active_flat = active.astype(jnp.float32)
    active_cells = jnp.broadcast_to(active_flat[None], pressure.shape)
    stacked = jnp.concatenate([conductivity, active_flat[None]], 0)
    widened = padded(stacked, ((GX, 1), (GY, 2)), 1)
    cond_ext = widened[:layers]
    act_ext = jnp.broadcast_to(widened[layers][None], cond_ext.shape)
    current = pressure
    leftover = jnp.zeros_like(pressure)
    for newton_index in range(NEWTON):
        diagonal = porosity * sat_slope(current)
        current_ext = padded(current, ((GX, 1), (GY, 2)), 1)
        faces = coefficients(current_ext, cond_ext, act_ext)
        remainder = -newton_residual(
            current_ext, faces, pressure_old, porosity, recharge, active_cells
        )
        first_norm = jnp.sqrt(by_axis(jnp.sum(remainder * remainder), GX_GY) + epsilon)
        basis_one = remainder / first_norm
        basis_ext = padded(basis_one, ((GX, 1), (GY, 2)), 1)
        image_one = jacobian_apply(basis_ext, faces, diagonal, active_cells)
        entry_one, square_one = (
            by_axis(jnp.sum(image_one * basis_one), GX_GY),
            by_axis(jnp.sum(image_one * image_one), GX_GY),
        )
        ortho_one = image_one - entry_one * basis_one
        entry_two = jnp.sqrt(square_one - entry_one * entry_one + epsilon)
        basis_two = ortho_one / entry_two
        second_ext = padded(basis_two, ((GX, 1), (GY, 2)), 1)
        image_two = jacobian_apply(second_ext, faces, diagonal, active_cells)
        entry_three, entry_four, square_two = (
            by_axis(jnp.sum(image_two * basis_one), GX_GY),
            by_axis(jnp.sum(image_two * basis_two), GX_GY),
            by_axis(jnp.sum(image_two * image_two), GX_GY),
        )
        entry_five = jnp.sqrt(
            square_two - entry_three * entry_three - entry_four * entry_four + epsilon
        )
        weight_one, weight_two = least_squares(
            first_norm, entry_one, entry_two, entry_three, entry_four, entry_five
        )
        current = current + (weight_one * basis_one + weight_two * basis_two)
        leftover = remainder - weight_one * image_one - weight_two * image_two
    return (current, leftover)


def solution(mesh):
    torus = Mesh(mesh.devices.reshape(4, 4, 4, 2), ("gx_0", "gx_1", "gy_0", "gy_1"))
    in_specs = (
        P(None, GX, GY),
        P(None, GX, GY),
        P(None, GX, GY),
        P(None, GX, GY),
        P(GX, GY),
        P(GX, GY),
    )
    out_specs = (P(None, GX, GY), P(None, GX, GY))
    return jax.shard_map(body, mesh=torus, in_specs=in_specs, out_specs=out_specs, check_vma=False)
```

profile of v0, /device:TPU:1, one launch (start us, length us, event | category | flops | bytes accessed | tf_op | source)
XLA Modules:
  0.0 389.7 jit_solution(7502140902498342127)
XLA Ops:
  3.4 3.9 %collective-permute-start = (f32[11,1,512]{2,1,0:T(1,128)}, f32[11,1,512]{2,1,0:T(1,128)S(1)}, u32[]{:S(2)}, u32[]{:S(2)}) collective-permute-start(f32[11,1,512]{2,1,0:T(1,128)} %get-tuple-element.72), channel_id=1, source_target_pairs={{0,8},{8,16},{16,24},{24,32},{32,40},{40,48},{48,56},{56,64},{64,7... | collective-permute-start | bytes 67592 | tf_op jit(solution)/shard_map/ppermute | solution.py:24
  9.0 4.0 %collective-permute-start.2 = (f32[11,64,1]{2,1,0:T(8,128)S(1)}, f32[11,64,1]{2,1,0:T(8,128)S(1)}, u32[]{:S(2)}, u32[]{:S(2)}) collective-permute-start(f32[11,64,1]{2,1,0:T(8,128)S(1)} %get-tuple-element.74), channel_id=1, source_target_pairs={{0,1},{1,2},{2,3},{3,4},{4,5},{5,6},{6,7},{8,9},{9,10},{10,11},{11... | collective-permute-start | bytes 8456 | tf_op jit(solution)/shard_map/ppermute | solution.py:24
  18.5 4.9 %collective-permute-start.4 = (f32[10,1,512]{2,1,0:T(1,128)S(1)}, f32[10,1,512]{2,1,0:T(1,128)S(1)}, u32[]{:S(2)}, u32[]{:S(2)}) collective-permute-start(f32[10,1,512]{2,1,0:T(1,128)S(1)} %get-tuple-element.98), channel_id=1, source_target_pairs={{0,8},{8,16},{16,24},{24,32},{32,40},{40,48},{48,56},{56,64},{64,7... | collective-permute-start | bytes 61448 | tf_op jit(solution)/shard_map/ppermute | solution.py:24
  23.4 3.9 %collective-permute-start.6 = (f32[10,64,1]{2,1,0:T(8,128)}, f32[10,64,1]{2,1,0:T(8,128)}, u32[]{:S(2)}, u32[]{:S(2)}) collective-permute-start(f32[10,64,1]{2,1,0:T(8,128)} %get-tuple-element.96), channel_id=1, source_target_pairs={{0,1},{1,2},{2,3},{3,4},{4,5},{5,6},{6,7},{8,9},{9,10},{10,11},{11... | collective-permute-start | bytes 7688 | tf_op jit(solution)/shard_map/ppermute | solution.py:24
  36.9 5.1 %multiply_multiply_fusion.1 = (f32[10,64,513]{2,1,0:T(8,128)S(1)}, f32[10,64,513]{2,1,0:T(8,128)}) fusion(f32[10,64,1]{2,1,0:T(8,128)} %collective-permute-done.7, f32[10,1,512]{2,1,0:T(1,128)S(1)} %collective-permute-done.5, f32[10,64,512]{2,1,0:T(8,128)S(1)} %copy-done, f32[10,1,512]{2,1,0:T(1,128)S(1)} %collective-permute-done.4, ...), kind=kLoop, calls=%fused_computation.83 | loop fusion | flops 11162880 | bytes 5738672 | tf_op jit(solution)/shard_map/mul | solution.py:63
  42.1 2.9 multiply_reduce_fusion.11
  45.0 13.0 %psum.336 = f32[]{:T(128)} all-reduce(f32[]{:T(128)} %get-tuple-element.66), channel_id=1, replica_groups=mesh['gx_0'=4,'gx_1'=4,'gy_0'=4,'gy_1'=2] {'gx_0'}, use_global_device_ids=true, to_apply=%region_1.2 | all-reduce | flops 1 | bytes 8 | tf_op jit(solution)/shard_map/psum | solution.py:38
  57.9 7.2 %psum.337 = f32[]{:T(128)} all-reduce(f32[]{:T(128)} %psum.336), channel_id=1, replica_groups=mesh['gx_0'=4,'gx_1'=4,'gy_0'=4,'gy_1'=2] {'gx_1'}, use_global_device_ids=true, to_apply=%region_2.3 | all-reduce | flops 1 | bytes 8 | tf_op jit(solution)/shard_map/psum | solution.py:38
  65.1 8.0 %psum.338 = f32[]{:T(128)} all-reduce(f32[]{:T(128)} %psum.337), channel_id=1, replica_groups=mesh['gx_0'=4,'gx_1'=4,'gy_0'=4,'gy_1'=2] {'gy_0'}, use_global_device_ids=true, to_apply=%region_3.4 | all-reduce | flops 1 | bytes 8 | tf_op jit(solution)/shard_map/psum | solution.py:38
  73.1 9.5 %psum.339 = f32[]{:T(128)} all-reduce(f32[]{:T(128)} %psum.338), channel_id=1, replica_groups=mesh['gx_0'=4,'gx_1'=4,'gy_0'=4,'gy_1'=2] {'gy_1'}, use_global_device_ids=true, to_apply=%region_4.5 | all-reduce | flops 1 | bytes 8 | tf_op jit(solution)/shard_map/psum | solution.py:38
  85.1 3.0 collective-permute-start.8
  95.1 3.1 fusion.30
  99.7 4.4 %fusion.19 = (f32[10,64,513]{2,1,0:T(8,128)S(1)}, f32[10,64,513]{2,1,0:T(8,128)}, f32[10,64,513]{2,1,0:T(8,128)}) fusion(f32[10,64,1]{2,1,0:T(8,128)S(1)} %collective-permute-done.11, f32[10,1,512]{2,1,0:T(1,128)S(1)} %collective-permute-done.9, f32[10,64,512]{2,1,0:T(8,128)S(1)} %negate_divide_fusion, f32[10,1,512]{2,1,0:T(1,128)S(1)} %collective-permute-done.8, ...), kind=kLoop, calls=%fused_computation.46 | loop fusion | flops 13789440 | bytes 7966720 | tf_op jit(solution)/shard_map/add | solution.py:114
  104.2 3.0 multiply_reduce_fusion.10
  107.1 10.9 %all-reduce.38 = (f32[]{:T(128)}, f32[]{:T(128)}) all-reduce(f32[]{:T(128)} %get-tuple-element.11, f32[]{:T(128)} %get-tuple-element.10), channel_id=1, replica_groups=mesh['gx_0'=4,'gx_1'=4,'gy_0'=4,'gy_1'=2] {'gx_0'}, use_global_device_ids=true, to_apply=%region_11.12 | all-reduce | flops 2 | bytes 16 | tf_op jit(solution)/shard_map/psum | solution.py:38
  118.1 6.7 %all-reduce.34 = (f32[]{:T(128)}, f32[]{:T(128)}) all-reduce(f32[]{:T(128)} %get-tuple-element.40, f32[]{:T(128)} %get-tuple-element.41), channel_id=1, replica_groups=mesh['gx_0'=4,'gx_1'=4,'gy_0'=4,'gy_1'=2] {'gx_1'}, use_global_device_ids=true, to_apply=%region_12.13 | all-reduce | flops 2 | bytes 16 | tf_op jit(solution)/shard_map/psum | solution.py:38
  124.8 7.6 %all-reduce.30 = (f32[]{:T(128)}, f32[]{:T(128)}) all-reduce(f32[]{:T(128)} %get-tuple-element.30, f32[]{:T(128)} %get-tuple-element.31), channel_id=1, replica_groups=mesh['gx_0'=4,'gx_1'=4,'gy_0'=4,'gy_1'=2] {'gy_0'}, use_global_device_ids=true, to_apply=%region_13.14 | all-reduce | flops 2 | bytes 16 | tf_op jit(solution)/shard_map/psum | solution.py:38
  132.4 7.7 %all-reduce.42 = (f32[]{:T(128)}, f32[]{:T(128)}) all-reduce(f32[]{:T(128)} %get-tuple-element.20, f32[]{:T(128)} %get-tuple-element.21), channel_id=1, replica_groups=mesh['gx_0'=4,'gx_1'=4,'gy_0'=4,'gy_1'=2] {'gy_1'}, use_global_device_ids=true, to_apply=%region_14.15 | all-reduce | flops 2 | bytes 16 | tf_op jit(solution)/shard_map/psum | solution.py:38
  146.6 3.6 collective-permute-start.12
  160.8 3.7 collective-permute-done.15
  168.7 10.3 %all-reduce.37 = (f32[]{:T(128)}, f32[]{:T(128)}, f32[]{:T(128)}) all-reduce(f32[]{:T(128)} %get-tuple-element.8, f32[]{:T(128)} %get-tuple-element.9, f32[]{:T(128)} %get-tuple-element.7), channel_id=1, replica_groups=mesh['gx_0'=4,'gx_1'=4,'gy_0'=4,'gy_1'=2] {'gx_0'}, use_global_device_ids=true, to_apply=%region_21.22 | all-reduce | flops 3 | bytes 24 | tf_op jit(solution)/shard_map/psum | solution.py:38
  179.0 6.7 %all-reduce.33 = (f32[]{:T(128)}, f32[]{:T(128)}, f32[]{:T(128)}) all-reduce(f32[]{:T(128)} %get-tuple-element.37, f32[]{:T(128)} %get-tuple-element.38, f32[]{:T(128)} %get-tuple-element.39), channel_id=1, replica_groups=mesh['gx_0'=4,'gx_1'=4,'gy_0'=4,'gy_1'=2] {'gx_1'}, use_global_device_ids=true, to_apply=%region_22.23 | all-reduce | flops 3 | bytes 24 | tf_op jit(solution)/shard_map/psum | solution.py:38
  185.7 6.7 %all-reduce.29 = (f32[]{:T(128)}, f32[]{:T(128)}, f32[]{:T(128)}) all-reduce(f32[]{:T(128)} %get-tuple-element.27, f32[]{:T(128)} %get-tuple-element.28, f32[]{:T(128)} %get-tuple-element.29), channel_id=1, replica_groups=mesh['gx_0'=4,'gx_1'=4,'gy_0'=4,'gy_1'=2] {'gy_0'}, use_global_device_ids=true, to_apply=%region_23.24 | all-reduce | flops 3 | bytes 24 | tf_op jit(solution)/shard_map/psum | solution.py:38
  192.4 8.5 %all-reduce.41 = (f32[]{:T(128)}, f32[]{:T(128)}, f32[]{:T(128)}) all-reduce(f32[]{:T(128)} %get-tuple-element.17, f32[]{:T(128)} %get-tuple-element.18, f32[]{:T(128)} %get-tuple-element.19), channel_id=1, replica_groups=mesh['gx_0'=4,'gx_1'=4,'gy_0'=4,'gy_1'=2] {'gy_1'}, use_global_device_ids=true, to_apply=%region_24.25 | all-reduce | flops 3 | bytes 24 | tf_op jit(solution)/shard_map/psum | solution.py:38
  209.8 3.8 collective-permute-start.16
  221.0 4.5 %collective-permute-done.19 = f32[10,64,1]{2,1,0:T(8,128)S(1)} collective-permute-done((f32[10,64,1]{2,1,0:T(8,128)S(1)}, f32[10,64,1]{2,1,0:T(8,128)S(1)}, u32[]{:S(2)}, u32[]{:S(2)}) %collective-permute-start.19) | collective-permute-done | bytes 2592 | tf_op jit(solution)/shard_map/ppermute | solution.py:25
  226.9 2.9 multiply_reduce_fusion.5
  229.7 9.8 %psum.360 = f32[]{:T(128)} all-reduce(f32[]{:T(128)} %get-tuple-element.57), channel_id=1, replica_groups=mesh['gx_0'=4,'gx_1'=4,'gy_0'=4,'gy_1'=2] {'gx_0'}, use_global_device_ids=true, to_apply=%region_31.32 | all-reduce | flops 1 | bytes 8 | tf_op jit(solution)/shard_map/psum | solution.py:38
  239.5 6.7 %psum.361 = f32[]{:T(128)} all-reduce(f32[]{:T(128)} %psum.360), channel_id=1, replica_groups=mesh['gx_0'=4,'gx_1'=4,'gy_0'=4,'gy_1'=2] {'gx_1'}, use_global_device_ids=true, to_apply=%region_32.33 | all-reduce | flops 1 | bytes 8 | tf_op jit(solution)/shard_map/psum | solution.py:38
  246.2 7.4 %psum.362 = f32[]{:T(128)} all-reduce(f32[]{:T(128)} %psum.361), channel_id=1, replica_groups=mesh['gx_0'=4,'gx_1'=4,'gy_0'=4,'gy_1'=2] {'gy_0'}, use_global_device_ids=true, to_apply=%region_33.34 | all-reduce | flops 1 | bytes 8 | tf_op jit(solution)/shard_map/psum | solution.py:38
  253.6 7.7 %psum.363 = f32[]{:T(128)} all-reduce(f32[]{:T(128)} %psum.362), channel_id=1, replica_groups=mesh['gx_0'=4,'gx_1'=4,'gy_0'=4,'gy_1'=2] {'gy_1'}, use_global_device_ids=true, to_apply=%region_34.35 | all-reduce | flops 1 | bytes 8 | tf_op jit(solution)/shard_map/psum | solution.py:38
  264.5 3.6 collective-permute-start.20
  276.4 4.4 %collective-permute-done.23 = f32[10,64,1]{2,1,0:T(8,128)S(1)} collective-permute-done((f32[10,64,1]{2,1,0:T(8,128)S(1)}, f32[10,64,1]{2,1,0:T(8,128)S(1)}, u32[]{:S(2)}, u32[]{:S(2)}) %collective-permute-start.23) | collective-permute-done | bytes 2592 | tf_op jit(solution)/shard_map/ppermute | solution.py:25
  280.8 3.3 fusion.7
  284.1 2.9 multiply_reduce_fusion.4
  287.1 10.3 %all-reduce.36 = (f32[]{:T(128)}, f32[]{:T(128)}) all-reduce(f32[]{:T(128)} %get-tuple-element.6, f32[]{:T(128)} %get-tuple-element.5), channel_id=1, replica_groups=mesh['gx_0'=4,'gx_1'=4,'gy_0'=4,'gy_1'=2] {'gx_0'}, use_global_device_ids=true, to_apply=%region_41.42 | all-reduce | flops 2 | bytes 16 | tf_op jit(solution)/shard_map/psum | solution.py:38
  297.4 6.7 %all-reduce.32 = (f32[]{:T(128)}, f32[]{:T(128)}) all-reduce(f32[]{:T(128)} %get-tuple-element.35, f32[]{:T(128)} %get-tuple-element.36), channel_id=1, replica_groups=mesh['gx_0'=4,'gx_1'=4,'gy_0'=4,'gy_1'=2] {'gx_1'}, use_global_device_ids=true, to_apply=%region_42.43 | all-reduce | flops 2 | bytes 16 | tf_op jit(solution)/shard_map/psum | solution.py:38
  304.1 6.7 %all-reduce.28 = (f32[]{:T(128)}, f32[]{:T(128)}) all-reduce(f32[]{:T(128)} %get-tuple-element.25, f32[]{:T(128)} %get-tuple-element.26), channel_id=1, replica_groups=mesh['gx_0'=4,'gx_1'=4,'gy_0'=4,'gy_1'=2] {'gy_0'}, use_global_device_ids=true, to_apply=%region_43.44 | all-reduce | flops 2 | bytes 16 | tf_op jit(solution)/shard_map/psum | solution.py:38
  310.8 8.5 %all-reduce.40 = (f32[]{:T(128)}, f32[]{:T(128)}) all-reduce(f32[]{:T(128)} %get-tuple-element.15, f32[]{:T(128)} %get-tuple-element.16), channel_id=1, replica_groups=mesh['gx_0'=4,'gx_1'=4,'gy_0'=4,'gy_1'=2] {'gy_1'}, use_global_device_ids=true, to_apply=%region_44.45 | all-reduce | flops 2 | bytes 16 | tf_op jit(solution)/shard_map/psum | solution.py:38
  325.9 3.6 collective-permute-start.24
  334.5 3.1 collective-permute-start.27
  337.7 3.3 fusion.33
  345.5 2.9 multiply_reduce_fusion
  348.4 9.8 %all-reduce.35 = (f32[]{:T(128)}, f32[]{:T(128)}, f32[]{:T(128)}) all-reduce(f32[]{:T(128)} %get-tuple-element.3, f32[]{:T(128)} %get-tuple-element.4, f32[]{:T(128)} %get-tuple-element.2), channel_id=1, replica_groups=mesh['gx_0'=4,'gx_1'=4,'gy_0'=4,'gy_1'=2] {'gx_0'}, use_global_device_ids=true, to_apply=%region_51.52 | all-reduce | flops 3 | bytes 24 | tf_op jit(solution)/shard_map/psum | solution.py:38
  358.3 6.6 %all-reduce.31 = (f32[]{:T(128)}, f32[]{:T(128)}, f32[]{:T(128)}) all-reduce(f32[]{:T(128)} %get-tuple-element.32, f32[]{:T(128)} %get-tuple-element.33, f32[]{:T(128)} %get-tuple-element.34), channel_id=1, replica_groups=mesh['gx_0'=4,'gx_1'=4,'gy_0'=4,'gy_1'=2] {'gx_1'}, use_global_device_ids=true, to_apply=%region_52.53 | all-reduce | flops 3 | bytes 24 | tf_op jit(solution)/shard_map/psum | solution.py:38
  364.9 7.5 %all-reduce.27 = (f32[]{:T(128)}, f32[]{:T(128)}, f32[]{:T(128)}) all-reduce(f32[]{:T(128)} %get-tuple-element.22, f32[]{:T(128)} %get-tuple-element.23, f32[]{:T(128)} %get-tuple-element.24), channel_id=1, replica_groups=mesh['gx_0'=4,'gx_1'=4,'gy_0'=4,'gy_1'=2] {'gy_0'}, use_global_device_ids=true, to_apply=%region_53.54 | all-reduce | flops 3 | bytes 24 | tf_op jit(solution)/shard_map/psum | solution.py:38
  372.4 7.7 %all-reduce.39 = (f32[]{:T(128)}, f32[]{:T(128)}, f32[]{:T(128)}) all-reduce(f32[]{:T(128)} %get-tuple-element.12, f32[]{:T(128)} %get-tuple-element.13, f32[]{:T(128)} %get-tuple-element.14), channel_id=1, replica_groups=mesh['gx_0'=4,'gx_1'=4,'gy_0'=4,'gy_1'=2] {'gy_1'}, use_global_device_ids=true, to_apply=%region_54.55 | all-reduce | flops 3 | bytes 24 | tf_op jit(solution)/shard_map/psum | solution.py:38
  385.3 4.4 %multiply_subtract_fusion = (f32[10,64,512]{2,1,0:T(8,128)}, f32[10,64,512]{2,1,0:T(8,128)}) fusion(f32[10,64,512]{2,1,0:T(8,128)} %get-tuple-element.52, f32[10,64,512]{2,1,0:T(8,128)} %get-tuple-element.53, f32[10,64,512]{2,1,0:T(8,128)} %get-tuple-element.58, f32[]{:T(128)S(6)} %div.125, f32[]{:T(128)S(6)} %div.126, ...), kind=kLoop, calls=%fused_computation.169 | loop fusion | flops 3276800 | bytes 9175052 | tf_op jit(solution)/shard_map/sub | solution.py:181
  (176 shorter events, 83.5 us)
Async XLA Ops:
  0.6 8.2 %copy-start.1 = (f32[10,64,512]{2,1,0:T(8,128)S(1)}, f32[10,64,512]{2,1,0:T(8,128)}, u32[]{:S(2)}) copy-start(f32[10,64,512]{2,1,0:T(8,128)} %param.8) | copy-start | bytes 3932164
  1.7 13.3 %copy-start = (f32[10,64,512]{2,1,0:T(8,128)S(1)}, f32[10,64,512]{2,1,0:T(8,128)}, u32[]{:S(2)}) copy-start(f32[10,64,512]{2,1,0:T(8,128)} %param.6) | copy-start | bytes 3932164
  3.4 28.3 %collective-permute-start = (f32[11,1,512]{2,1,0:T(1,128)}, f32[11,1,512]{2,1,0:T(1,128)S(1)}, u32[]{:S(2)}, u32[]{:S(2)}) collective-permute-start(f32[11,1,512]{2,1,0:T(1,128)} %get-tuple-element.72), channel_id=1, source_target_pairs={{0,8},{8,16},{16,24},{24,32},{32,40},{40,48},{48,56},{56,64},{64,7... | collective-permute-start | bytes 67592 | tf_op jit(solution)/shard_map/ppermute | solution.py:24
  7.4 9.9 %copy-start.44 = (s32[64,512]{1,0:T(8,128)S(1)}, s32[64,512]{1,0:T(8,128)}, u32[]{:S(2)}) copy-start(s32[64,512]{1,0:T(8,128)} %param.11) | copy-start | bytes 393220
  7.4 24.4 %collective-permute-start.1 = (f32[11,1,512]{2,1,0:T(1,128)S(1)}, f32[11,1,512]{2,1,0:T(1,128)S(1)}, u32[]{:S(2)}, u32[]{:S(2)}) collective-permute-start(f32[11,1,512]{2,1,0:T(1,128)S(1)} %get-tuple-element.73), channel_id=1, source_target_pairs={{8,0},{16,8},{24,16},{32,24},{40,32},{48,40},{56,48},{64,56},{72,6... | collective-permute-start | bytes 67592 | tf_op jit(solution)/shard_map/ppermute | solution.py:25
  9.0 9.5 %collective-permute-start.2 = (f32[11,64,1]{2,1,0:T(8,128)S(1)}, f32[11,64,1]{2,1,0:T(8,128)S(1)}, u32[]{:S(2)}, u32[]{:S(2)}) collective-permute-start(f32[11,64,1]{2,1,0:T(8,128)S(1)} %get-tuple-element.74), channel_id=1, source_target_pairs={{0,1},{1,2},{2,3},{3,4},{4,5},{5,6},{6,7},{8,9},{9,10},{10,11},{11... | collective-permute-start | bytes 8456 | tf_op jit(solution)/shard_map/ppermute | solution.py:24
  13.1 10.4 %collective-permute-start.3 = (f32[11,64,1]{2,1,0:T(8,128)S(1)}, f32[11,64,1]{2,1,0:T(8,128)S(1)}, u32[]{:S(2)}, u32[]{:S(2)}) collective-permute-start(f32[11,64,1]{2,1,0:T(8,128)S(1)} %get-tuple-element.75), channel_id=1, source_target_pairs={{1,0},{2,1},{3,2},{4,3},{5,4},{6,5},{7,6},{9,8},{10,9},{11,10},{12... | collective-permute-start | bytes 8456 | tf_op jit(solution)/shard_map/ppermute | solution.py:25
  15.0 13.1 %collective-permute-start.5 = (f32[10,1,512]{2,1,0:T(1,128)S(1)}, f32[10,1,512]{2,1,0:T(1,128)S(1)}, u32[]{:S(2)}, u32[]{:S(2)}) collective-permute-start(f32[10,1,512]{2,1,0:T(1,128)S(1)} %get-tuple-element.99), channel_id=1, source_target_pairs={{8,0},{16,8},{24,16},{32,24},{40,32},{48,40},{56,48},{64,56},{72,6... | collective-permute-start | bytes 61448 | tf_op jit(solution)/shard_map/ppermute | solution.py:25
  18.5 16.1 %collective-permute-start.4 = (f32[10,1,512]{2,1,0:T(1,128)S(1)}, f32[10,1,512]{2,1,0:T(1,128)S(1)}, u32[]{:S(2)}, u32[]{:S(2)}) collective-permute-start(f32[10,1,512]{2,1,0:T(1,128)S(1)} %get-tuple-element.98), channel_id=1, source_target_pairs={{0,8},{8,16},{16,24},{24,32},{32,40},{40,48},{48,56},{56,64},{64,7... | collective-permute-start | bytes 61448 | tf_op jit(solution)/shard_map/ppermute | solution.py:24
  23.4 9.2 %copy-start.35 = (f32[11,66,1]{2,1,0:T(8,128)}, f32[11,66,1]{2,1,0:T(8,128)S(1)}, u32[]{:S(2)}) copy-start(f32[11,66,1]{2,1,0:T(8,128)S(1)} %pad.57) | copy-start | bytes 8716
  23.4 12.4 %collective-permute-start.6 = (f32[10,64,1]{2,1,0:T(8,128)}, f32[10,64,1]{2,1,0:T(8,128)}, u32[]{:S(2)}, u32[]{:S(2)}) collective-permute-start(f32[10,64,1]{2,1,0:T(8,128)} %get-tuple-element.96), channel_id=1, source_target_pairs={{0,1},{1,2},{2,3},{3,4},{4,5},{5,6},{6,7},{8,9},{9,10},{10,11},{11... | collective-permute-start | bytes 7688 | tf_op jit(solution)/shard_map/ppermute | solution.py:24
  28.2 8.7 %collective-permute-start.7 = (f32[10,64,1]{2,1,0:T(8,128)}, f32[10,64,1]{2,1,0:T(8,128)}, u32[]{:S(2)}, u32[]{:S(2)}) collective-permute-start(f32[10,64,1]{2,1,0:T(8,128)} %get-tuple-element.97), channel_id=1, source_target_pairs={{1,0},{2,1},{3,2},{4,3},{5,4},{6,5},{7,6},{9,8},{10,9},{11,10},{12... | collective-permute-start | bytes 7688 | tf_op jit(solution)/shard_map/ppermute | solution.py:25
  83.3 10.5 %copy-start.17 = (f32[9,64,512]{2,1,0:T(8,128)S(1)}, f32[9,64,512]{2,1,0:T(8,128)}, u32[]{:S(2)}) copy-start(f32[9,64,512]{2,1,0:T(8,128)} %get-tuple-element.69) | copy-start | bytes 3538948
  85.1 9.5 %collective-permute-start.8 = (f32[10,1,512]{2,1,0:T(1,128)S(1)}, f32[10,1,512]{2,1,0:T(1,128)S(1)}, u32[]{:S(2)}, u32[]{:S(2)}) collective-permute-start(f32[10,1,512]{2,1,0:T(1,128)S(1)} %get-tuple-element.94), channel_id=1, source_target_pairs={{0,8},{8,16},{16,24},{24,32},{32,40},{40,48},{48,56},{56,64},{64,7... | collective-permute-start | bytes 61448 | tf_op jit(solution)/shard_map/ppermute | solution.py:24
  88.1 6.5 %collective-permute-start.9 = (f32[10,1,512]{2,1,0:T(1,128)S(1)}, f32[10,1,512]{2,1,0:T(1,128)S(1)}, u32[]{:S(2)}, u32[]{:S(2)}) collective-permute-start(f32[10,1,512]{2,1,0:T(1,128)S(1)} %get-tuple-element.95), channel_id=1, source_target_pairs={{8,0},{16,8},{24,16},{32,24},{40,32},{48,40},{56,48},{64,56},{72,6... | collective-permute-start | bytes 61448 | tf_op jit(solution)/shard_map/ppermute | solution.py:25
  89.4 8.8 %collective-permute-start.10 = (f32[10,64,1]{2,1,0:T(8,128)S(1)}, f32[10,64,1]{2,1,0:T(8,128)S(1)}, u32[]{:S(2)}, u32[]{:S(2)}) collective-permute-start(f32[10,64,1]{2,1,0:T(8,128)S(1)} %get-tuple-element.92), channel_id=1, source_target_pairs={{0,1},{1,2},{2,3},{3,4},{4,5},{5,6},{6,7},{8,9},{9,10},{10,11},{11... | collective-permute-start | bytes 7688 | tf_op jit(solution)/shard_map/ppermute | solution.py:24
  91.3 8.4 %collective-permute-start.11 = (f32[10,64,1]{2,1,0:T(8,128)S(1)}, f32[10,64,1]{2,1,0:T(8,128)S(1)}, u32[]{:S(2)}, u32[]{:S(2)}) collective-permute-start(f32[10,64,1]{2,1,0:T(8,128)S(1)} %get-tuple-element.93), channel_id=1, source_target_pairs={{1,0},{2,1},{3,2},{4,3},{5,4},{6,5},{7,6},{9,8},{10,9},{11,10},{12... | collective-permute-start | bytes 7688 | tf_op jit(solution)/shard_map/ppermute | solution.py:25
  144.7 21.6 %copy-start.6 = (f32[10,64,512]{2,1,0:T(8,128)}, f32[10,64,512]{2,1,0:T(8,128)S(1)}, u32[]{:S(2)}) copy-start(f32[10,64,512]{2,1,0:T(8,128)S(1)} %subtract_divide_fusion.1) | copy-start | bytes 3932164
  146.6 11.6 %collective-permute-start.12 = (f32[10,1,512]{2,1,0:T(1,128)S(1)}, f32[10,1,512]{2,1,0:T(1,128)S(1)}, u32[]{:S(2)}, u32[]{:S(2)}) collective-permute-start(f32[10,1,512]{2,1,0:T(1,128)S(1)} %get-tuple-element.90), channel_id=1, source_target_pairs={{0,8},{8,16},{16,24},{24,32},{32,40},{40,48},{48,56},{56,64},{64,7... | collective-permute-start | bytes 61448 | tf_op jit(solution)/shard_map/ppermute | solution.py:24
  150.2 8.0 %collective-permute-start.13 = (f32[10,1,512]{2,1,0:T(1,128)S(1)}, f32[10,1,512]{2,1,0:T(1,128)S(1)}, u32[]{:S(2)}, u32[]{:S(2)}) collective-permute-start(f32[10,1,512]{2,1,0:T(1,128)S(1)} %get-tuple-element.91), channel_id=1, source_target_pairs={{8,0},{16,8},{24,16},{32,24},{40,32},{48,40},{56,48},{64,56},{72,6... | collective-permute-start | bytes 61448 | tf_op jit(solution)/shard_map/ppermute | solution.py:25
  153.1 7.6 %collective-permute-start.14 = (f32[10,64,1]{2,1,0:T(8,128)}, f32[10,64,1]{2,1,0:T(8,128)}, u32[]{:S(2)}, u32[]{:S(2)}) collective-permute-start(f32[10,64,1]{2,1,0:T(8,128)} %get-tuple-element.88), channel_id=1, source_target_pairs={{0,1},{1,2},{2,3},{3,4},{4,5},{5,6},{6,7},{8,9},{9,10},{10,11},{11... | collective-permute-start | bytes 7688 | tf_op jit(solution)/shard_map/ppermute | solution.py:24
  155.7 8.7 %collective-permute-start.15 = (f32[10,64,1]{2,1,0:T(8,128)}, f32[10,64,1]{2,1,0:T(8,128)}, u32[]{:S(2)}, u32[]{:S(2)}) collective-permute-start(f32[10,64,1]{2,1,0:T(8,128)} %get-tuple-element.89), channel_id=1, source_target_pairs={{1,0},{2,1},{3,2},{4,3},{5,4},{6,5},{7,6},{9,8},{10,9},{11,10},{12... | collective-permute-start | bytes 7688 | tf_op jit(solution)/shard_map/ppermute | solution.py:25
  158.2 6.2 %copy-start.29 = (f32[10,64,513]{2,1,0:T(8,128)S(1)}, f32[10,64,513]{2,1,0:T(8,128)}, u32[]{:S(2)}) copy-start(f32[10,64,513]{2,1,0:T(8,128)} %get-tuple-element.64) | copy-start | bytes 3939844
  158.2 6.2 %copy-start.30 = (f32[10,64,513]{2,1,0:T(8,128)S(1)}, f32[10,64,513]{2,1,0:T(8,128)}, u32[]{:S(2)}) copy-start(f32[10,64,513]{2,1,0:T(8,128)} %get-tuple-element.65) | copy-start | bytes 3939844
  209.8 9.8 %copy-start.2 = (f32[10,64,512]{2,1,0:T(8,128)S(1)}, f32[10,64,512]{2,1,0:T(8,128)}, u32[]{:S(2)}) copy-start(f32[10,64,512]{2,1,0:T(8,128)} %param.8) | copy-start | bytes 3932164
  209.8 9.8 %collective-permute-start.16 = (f32[10,1,512]{2,1,0:T(1,128)S(1)}, f32[10,1,512]{2,1,0:T(1,128)S(1)}, u32[]{:S(2)}, u32[]{:S(2)}) collective-permute-start(f32[10,1,512]{2,1,0:T(1,128)S(1)} %get-tuple-element.86), channel_id=1, source_target_pairs={{0,8},{8,16},{16,24},{24,32},{32,40},{40,48},{48,56},{56,64},{64,7... | collective-permute-start | bytes 61448 | tf_op jit(solution)/shard_map/ppermute | solution.py:24
  213.6 6.0 %collective-permute-start.17 = (f32[10,1,512]{2,1,0:T(1,128)S(1)}, f32[10,1,512]{2,1,0:T(1,128)S(1)}, u32[]{:S(2)}, u32[]{:S(2)}) collective-permute-start(f32[10,1,512]{2,1,0:T(1,128)S(1)} %get-tuple-element.87), channel_id=1, source_target_pairs={{8,0},{16,8},{24,16},{32,24},{40,32},{48,40},{56,48},{64,56},{72,6... | collective-permute-start | bytes 61448 | tf_op jit(solution)/shard_map/ppermute | solution.py:25
  215.1 5.9 %collective-permute-start.18 = (f32[10,64,1]{2,1,0:T(8,128)S(1)}, f32[10,64,1]{2,1,0:T(8,128)S(1)}, u32[]{:S(2)}, u32[]{:S(2)}) collective-permute-start(f32[10,64,1]{2,1,0:T(8,128)S(1)} %get-tuple-element.84), channel_id=1, source_target_pairs={{0,1},{1,2},{2,3},{3,4},{4,5},{5,6},{6,7},{8,9},{9,10},{10,11},{11... | collective-permute-start | bytes 7688 | tf_op jit(solution)/shard_map/ppermute | solution.py:24
  217.0 8.5 %copy-start.23 = (f32[10,64,513]{2,1,0:T(8,128)S(1)}, f32[10,64,513]{2,1,0:T(8,128)}, u32[]{:S(2)}) copy-start(f32[10,64,513]{2,1,0:T(8,128)} %get-tuple-element.71) | copy-start | bytes 3939844
  217.0 8.5 %collective-permute-start.19 = (f32[10,64,1]{2,1,0:T(8,128)S(1)}, f32[10,64,1]{2,1,0:T(8,128)S(1)}, u32[]{:S(2)}, u32[]{:S(2)}) collective-permute-start(f32[10,64,1]{2,1,0:T(8,128)S(1)} %get-tuple-element.85), channel_id=1, source_target_pairs={{1,0},{2,1},{3,2},{4,3},{5,4},{6,5},{7,6},{9,8},{10,9},{11,10},{12... | collective-permute-start | bytes 7688 | tf_op jit(solution)/shard_map/ppermute | solution.py:25
  220.8 6.0 %copy-start.10 = (f32[10,64,512]{2,1,0:T(8,128)S(1)}, f32[10,64,512]{2,1,0:T(8,128)}, u32[]{:S(2)}) copy-start(f32[10,64,512]{2,1,0:T(8,128)} %param.9) | copy-start | bytes 3932164
  220.8 6.0 %copy-start.32 = (f32[10,64,512]{2,1,0:T(8,128)S(1)}, f32[10,64,512]{2,1,0:T(8,128)}, u32[]{:S(2)}) copy-start(f32[10,64,512]{2,1,0:T(8,128)} %param.7) | copy-start | bytes 3932164
  220.9 6.0 %copy-start.43 = (f32[64,512]{1,0:T(8,128)S(1)}, f32[64,512]{1,0:T(8,128)}, u32[]{:S(2)}) copy-start(f32[64,512]{1,0:T(8,128)} %param.10) | copy-start | bytes 393220
  264.5 10.0 %collective-permute-start.20 = (f32[10,1,512]{2,1,0:T(1,128)S(1)}, f32[10,1,512]{2,1,0:T(1,128)S(1)}, u32[]{:S(2)}, u32[]{:S(2)}) collective-permute-start(f32[10,1,512]{2,1,0:T(1,128)S(1)} %get-tuple-element.82), channel_id=1, source_target_pairs={{0,8},{8,16},{16,24},{24,32},{32,40},{40,48},{48,56},{56,64},{64,7... | collective-permute-start | bytes 61448 | tf_op jit(solution)/shard_map/ppermute | solution.py:24
  268.1 6.4 %collective-permute-start.21 = (f32[10,1,512]{2,1,0:T(1,128)S(1)}, f32[10,1,512]{2,1,0:T(1,128)S(1)}, u32[]{:S(2)}, u32[]{:S(2)}) collective-permute-start(f32[10,1,512]{2,1,0:T(1,128)S(1)} %get-tuple-element.83), channel_id=1, source_target_pairs={{8,0},{16,8},{24,16},{32,24},{40,32},{48,40},{56,48},{64,56},{72,6... | collective-permute-start | bytes 61448 | tf_op jit(solution)/shard_map/ppermute | solution.py:25
  269.6 6.8 %collective-permute-start.22 = (f32[10,64,1]{2,1,0:T(8,128)S(1)}, f32[10,64,1]{2,1,0:T(8,128)S(1)}, u32[]{:S(2)}, u32[]{:S(2)}) collective-permute-start(f32[10,64,1]{2,1,0:T(8,128)S(1)} %get-tuple-element.80), channel_id=1, source_target_pairs={{0,1},{1,2},{2,3},{3,4},{4,5},{5,6},{6,7},{8,9},{9,10},{10,11},{11... | collective-permute-start | bytes 7688 | tf_op jit(solution)/shard_map/ppermute | solution.py:24
  272.2 8.6 %copy-start.24 = (f32[10,64,513]{2,1,0:T(8,128)S(1)}, f32[10,64,513]{2,1,0:T(8,128)}, u32[]{:S(2)}) copy-start(f32[10,64,513]{2,1,0:T(8,128)} %get-tuple-element.71) | copy-start | bytes 3939844
  272.2 8.6 %copy-start.39 = (f32[10,64,1]{2,1,0:T(8,128)S(1)}, f32[10,64,1]{2,1,0:T(8,128)}, u32[]{:S(2)}) copy-start(f32[10,64,1]{2,1,0:T(8,128)} %copy-done.38) | copy-start | bytes 7684
  272.3 8.5 %copy-start.41 = (f32[10,64,1]{2,1,0:T(8,128)S(1)}, f32[10,64,1]{2,1,0:T(8,128)}, u32[]{:S(2)}) copy-start(f32[10,64,1]{2,1,0:T(8,128)} %copy-done.40) | copy-start | bytes 7684
  272.3 8.5 %collective-permute-start.23 = (f32[10,64,1]{2,1,0:T(8,128)S(1)}, f32[10,64,1]{2,1,0:T(8,128)S(1)}, u32[]{:S(2)}, u32[]{:S(2)}) collective-permute-start(f32[10,64,1]{2,1,0:T(8,128)S(1)} %get-tuple-element.81), channel_id=1, source_target_pairs={{1,0},{2,1},{3,2},{4,3},{5,4},{6,5},{7,6},{9,8},{10,9},{11,10},{12... | collective-permute-start | bytes 7688 | tf_op jit(solution)/shard_map/ppermute | solution.py:25
  276.4 7.7 %copy-start.11 = (f32[10,64,512]{2,1,0:T(8,128)S(1)}, f32[10,64,512]{2,1,0:T(8,128)}, u32[]{:S(2)}) copy-start(f32[10,64,512]{2,1,0:T(8,128)} %param.9) | copy-start | bytes 3932164
  276.4 7.7 %copy-start.15 = (f32[10,64,512]{2,1,0:T(8,128)S(1)}, f32[10,64,512]{2,1,0:T(8,128)}, u32[]{:S(2)}) copy-start(f32[10,64,512]{2,1,0:T(8,128)} %get-tuple-element.58) | copy-start | bytes 3932164
  324.0 6.9 %copy-start.3 = (f32[10,64,512]{2,1,0:T(8,128)}, f32[10,64,512]{2,1,0:T(8,128)S(1)}, u32[]{:S(2)}) copy-start(f32[10,64,512]{2,1,0:T(8,128)S(1)} %subtract_divide_fusion) | copy-start | bytes 3932164
  325.9 11.7 %collective-permute-start.24 = (f32[10,1,512]{2,1,0:T(1,128)S(1)}, f32[10,1,512]{2,1,0:T(1,128)S(1)}, u32[]{:S(2)}, u32[]{:S(2)}) collective-permute-start(f32[10,1,512]{2,1,0:T(1,128)S(1)} %get-tuple-element.78), channel_id=1, source_target_pairs={{0,8},{8,16},{16,24},{24,32},{32,40},{40,48},{48,56},{56,64},{64,7... | collective-permute-start | bytes 61448 | tf_op jit(solution)/shard_map/ppermute | solution.py:24
  329.6 8.1 %collective-permute-start.25 = (f32[10,1,512]{2,1,0:T(1,128)S(1)}, f32[10,1,512]{2,1,0:T(1,128)S(1)}, u32[]{:S(2)}, u32[]{:S(2)}) collective-permute-start(f32[10,1,512]{2,1,0:T(1,128)S(1)} %get-tuple-element.79), channel_id=1, source_target_pairs={{8,0},{16,8},{24,16},{32,24},{40,32},{48,40},{56,48},{64,56},{72,6... | collective-permute-start | bytes 61448 | tf_op jit(solution)/shard_map/ppermute | solution.py:25
  332.6 8.4 %collective-permute-start.26 = (f32[10,64,1]{2,1,0:T(8,128)}, f32[10,64,1]{2,1,0:T(8,128)}, u32[]{:S(2)}, u32[]{:S(2)}) collective-permute-start(f32[10,64,1]{2,1,0:T(8,128)} %get-tuple-element.76), channel_id=1, source_target_pairs={{0,1},{1,2},{2,3},{3,4},{4,5},{5,6},{6,7},{8,9},{9,10},{10,11},{11... | collective-permute-start | bytes 7688 | tf_op jit(solution)/shard_map/ppermute | solution.py:24
  334.5 8.7 %collective-permute-start.27 = (f32[10,64,1]{2,1,0:T(8,128)}, f32[10,64,1]{2,1,0:T(8,128)}, u32[]{:S(2)}, u32[]{:S(2)}) collective-permute-start(f32[10,64,1]{2,1,0:T(8,128)} %get-tuple-element.77), channel_id=1, source_target_pairs={{1,0},{2,1},{3,2},{4,3},{5,4},{6,5},{7,6},{9,8},{10,9},{11,10},{12... | collective-permute-start | bytes 7688 | tf_op jit(solution)/shard_map/ppermute | solution.py:25
  345.5 39.8 %copy-start.5 = (f32[10,64,512]{2,1,0:T(8,128)S(1)}, f32[10,64,512]{2,1,0:T(8,128)}, u32[]{:S(2)}) copy-start(f32[10,64,512]{2,1,0:T(8,128)} %copy-done.3) | copy-start | bytes 3932164
  (25 other events, 82.7 us)
where the time goes:
time: 392 us; the launch traced here: 390 us
  blocking collectives  198 us (51%)
  other arithmetic  74.3 us (19%)
  starting transfers between devices  71.2 us (18%)
  between operations  19.5 us (5%)
  waiting for transfers between devices  17.5 us (4%)
  local copies, waits for them, and re-layouts  8.9 us (2%)
    psum x24, blocking collectives, by_axis(): value = lax.psum(value, axis)  198 us
    ppermute x14, starting transfers between devices, padded(): lax.ppermute(last, axis, up)  45.4 us
    ppermute x14, starting transfers between devices, padded(): lax.ppermute(initial, axis, [(b, a) for a, b in up])  25.8 us
    ppermute x14, waiting for transfers between devices, padded(): lax.ppermute(initial, axis, [(b, a) for a, b in up])  17.3 us
    add x4, other arithmetic, jacobian_apply(): flow_y = y_low * vector[:, 1:-1, :-1] + y_high * vector[:, 1:-1, 1:]  11.4 us
    mul x6, other arithmetic, face_pair(): return (coef_low, coef_high, transmit * mobility * head_drop)  10.8 us
    add x4, other arithmetic, jacobian_apply(): flow_x = x_low * vector[:, :-1, 1:-1] + x_high * vector[:, 1:, 1:-1]  10.7 us
  transfers between devices with their start and end apart: 28, of which 7 were waited for; matrix products, arithmetic and copies ran while one was open for 6% of the time, Pallas kernels for 0%

commit v1 on v0

--- a/solution.py
+++ b/solution.py
@@ -35,7 +35,11 @@
 
 def by_axis(value, axes):
     for axis in axes:
-        value = lax.psum(value, axis)
+
+        def wrap_ranges(in_array, axis_name):
+            return lax.all_gather(in_array, axis_name=axis_name).sum(axis=0)
+
+        value = wrap_ranges(value, axis)
     return value
 
 

time: 392 us -> 488 us (1.24); the launches traced: 390 us -> 479 us
  local copies, waits for them, and re-layouts: 8.9 us -> 83.8 us
  other arithmetic: 74.3 us -> 104 us
  blocking collectives: 198 us -> 182 us
    psum x24 -> x0, blocking collectives: 198 us -> none  [by_axis(): value = lax.psum(value, axis)]
    unnamed x0 -> x24, blocking collectives: none -> 182 us
    unnamed x91 -> x199, local copies, waits for them, and re-layouts: 2.73 us -> 75.1 us
    reduce_sum x0 -> x48, other arithmetic: none -> 31.3 us  [wrap_ranges(): return lax.all_gather(in_array, axis_name=axis_name).sum(axis=0)]
where the time goes in v1:
time: 488 us; the launch traced here: 479 us
  blocking collectives  182 us (37%)
  other arithmetic  104 us (21%)
  local copies, waits for them, and re-layouts  83.8 us (17%)
  starting transfers between devices  70.4 us (14%)
  between operations  20.2 us (4%)
  waiting for transfers between devices  18.5 us (4%)
    unnamed x24, blocking collectives  182 us
    unnamed x199, local copies, waits for them, and re-layouts  75.1 us
    ppermute x14, starting transfers between devices, padded(): lax.ppermute(last, axis, up)  45.3 us
    reduce_sum x48, other arithmetic, wrap_ranges(): return lax.all_gather(in_array, axis_name=axis_name).sum(axis=0)  31.3 us
    ppermute x14, starting transfers between devices, padded(): lax.ppermute(initial, axis, [(b, a) for a, b in up])  25.1 us
    ppermute x14, waiting for transfers between devices, padded(): lax.ppermute(initial, axis, [(b, a) for a, b in up])  18.3 us
    mul x6, other arithmetic, face_pair(): return (coef_low, coef_high, transmit * mobility * head_drop)  10.8 us
    add x4, other arithmetic, jacobian_apply(): flow_x = x_low * vector[:, :-1, 1:-1] + x_high * vector[:, 1:, 1:-1]  10.5 us
  transfers between devices with their start and end apart: 28, of which 7 were waited for; matrix products, arithmetic and copies ran while one was open for 6% of the time, Pallas kernels for 0%

profile of v1, /device:TPU:1, one launch (start us, length us, event | category | flops | bytes accessed | tf_op | source)
XLA Modules:
  0.0 479.3 jit_solution(8946434409775386232)
XLA Ops:
  3.4 3.9 collective-permute-start
  9.8 4.0 collective-permute-start.2
  20.4 4.9 %collective-permute-start.4 = (f32[10,1,512]{2,1,0:T(1,128)S(1)}, f32[10,1,512]{2,1,0:T(1,128)S(1)}, u32[]{:S(2)}, u32[]{:S(2)}) collective-permute-start(f32[10,1,512]{2,1,0:T(1,128)S(1)} %get-tuple-element.98), channel_id=1, source_target_pairs={{0,8},{8,16},{16,24},{24,32},{32,40},{40,48},{48,56},{56,64},{64,7... | collective-permute-start | bytes 61448 | tf_op jit(solution)/shard_map/ppermute | solution.py:24
  26.4 3.9 collective-permute-start.6
  40.8 5.1 %multiply_multiply_fusion.1 = (f32[10,64,513]{2,1,0:T(8,128)S(1)}, f32[10,64,513]{2,1,0:T(8,128)}) fusion(f32[10,64,1]{2,1,0:T(8,128)} %collective-permute-done.7, f32[10,1,512]{2,1,0:T(1,128)S(1)} %collective-permute-done.5, f32[10,64,512]{2,1,0:T(8,128)S(1)} %copy-done, f32[10,1,512]{2,1,0:T(1,128)S(1)} %collective-permute-done.4, ...), kind=kLoop, calls=%fused_computation.83 | loop fusion | flops 11162880 | bytes 5738672 | tf_op jit(solution)/shard_map/mul | solution.py:67
  46.0 2.9 multiply_reduce_fusion.11
  50.9 12.4 %all-reduce.27 = f32[4]{0:T(128)S(1)} all-reduce(f32[4]{0:T(128)S(1)} %dynamic-update-slice), channel_id=1, replica_groups=mesh['gx_0'=4,'gx_1'=4,'gy_0'=4,'gy_1'=2] {'gx_0'}, use_global_device_ids=true, to_apply=%add.27 | all-reduce | flops 4 | bytes 32
  66.0 6.6 %all-reduce.28 = f32[4]{0:T(128)S(1)} all-reduce(f32[4]{0:T(128)S(1)} %dynamic-update-slice.1), channel_id=1, replica_groups=mesh['gx_0'=4,'gx_1'=4,'gy_0'=4,'gy_1'=2] {'gx_1'}, use_global_device_ids=true, to_apply=%add.28 | all-reduce | flops 4 | bytes 32
  75.2 7.0 %all-reduce.29 = f32[4]{0:T(128)S(1)} all-reduce(f32[4]{0:T(128)S(1)} %dynamic-update-slice.2), channel_id=1, replica_groups=mesh['gx_0'=4,'gx_1'=4,'gy_0'=4,'gy_1'=2] {'gy_0'}, use_global_device_ids=true, to_apply=%add.29 | all-reduce | flops 4 | bytes 32
  84.1 9.2 %all-reduce.30 = f32[2]{0:T(128)S(1)} all-reduce(f32[2]{0:T(128)S(1)} %dynamic-update-slice.3), channel_id=1, replica_groups=mesh['gx_0'=4,'gx_1'=4,'gy_0'=4,'gy_1'=2] {'gy_1'}, use_global_device_ids=true, to_apply=%add.30 | all-reduce | flops 2 | bytes 16
  96.4 3.0 collective-permute-start.8
  106.9 3.0 fusion.30
  111.1 4.4 fusion.19
  115.5 2.9 multiply_reduce_fusion.10
  121.2 10.1 %all-reduce.86 = (f32[4]{0:T(128)S(1)}, f32[4]{0:T(128)S(1)}) all-reduce(f32[4]{0:T(128)S(1)} %dynamic-update-slice.8, f32[4]{0:T(128)S(1)} %dynamic-update-slice.4), channel_id=1, replica_groups=mesh['gx_0'=4,'gx_1'=4,'gy_0'=4,'gy_1'=2] {'gx_0'}, use_global_device_ids=true, to_apply=%add.35 | all-reduce | flops 8 | bytes 64
  135.6 6.0 %all-reduce.82 = (f32[4]{0:T(128)S(1)}, f32[4]{0:T(128)S(1)}) all-reduce(f32[4]{0:T(128)S(1)} %dynamic-update-slice.9, f32[4]{0:T(128)S(1)} %dynamic-update-slice.5), channel_id=1, replica_groups=mesh['gx_0'=4,'gx_1'=4,'gy_0'=4,'gy_1'=2] {'gx_1'}, use_global_device_ids=true, to_apply=%add.36 | all-reduce | flops 8 | bytes 64
  145.9 6.9 %all-reduce.78 = (f32[4]{0:T(128)S(1)}, f32[4]{0:T(128)S(1)}) all-reduce(f32[4]{0:T(128)S(1)} %dynamic-update-slice.10, f32[4]{0:T(128)S(1)} %dynamic-update-slice.6), channel_id=1, replica_groups=mesh['gx_0'=4,'gx_1'=4,'gy_0'=4,'gy_1'=2] {'gy_0'}, use_global_device_ids=true, to_apply=%add.37 | all-reduce | flops 8 | bytes 64
  157.0 7.3 %all-reduce.90 = (f32[2]{0:T(128)S(1)}, f32[2]{0:T(128)S(1)}) all-reduce(f32[2]{0:T(128)S(1)} %dynamic-update-slice.11, f32[2]{0:T(128)S(1)} %dynamic-update-slice.7), channel_id=1, replica_groups=mesh['gx_0'=4,'gx_1'=4,'gy_0'=4,'gy_1'=2] {'gy_1'}, use_global_device_ids=true, to_apply=%add.38 | all-reduce | flops 4 | bytes 32
  172.3 3.6 collective-permute-start.12
  185.2 4.1 collective-permute-done.15
  197.5 9.3 %all-reduce.85 = (f32[4]{0:T(128)S(1)}, f32[4]{0:T(128)S(1)}, f32[4]{0:T(128)S(1)}) all-reduce(f32[4]{0:T(128)S(1)} %dynamic-update-slice.16, f32[4]{0:T(128)S(1)} %dynamic-update-slice.12, f32[4]{0:T(128)S(1)} %dynamic-update-slice.20), channel_id=1, replica_groups=mesh['gx_0'=4,'gx_1'=4,'gy_0'=4,'gy_1'=2] {'gx_0'}, use_global_device_ids=true, to_apply=%add.43 | all-reduce | flops 12 | bytes 96
  213.2 6.0 %all-reduce.81 = (f32[4]{0:T(128)S(1)}, f32[4]{0:T(128)S(1)}, f32[4]{0:T(128)S(1)}) all-reduce(f32[4]{0:T(128)S(1)} %dynamic-update-slice.17, f32[4]{0:T(128)S(1)} %dynamic-update-slice.13, f32[4]{0:T(128)S(1)} %dynamic-update-slice.21), channel_id=1, replica_groups=mesh['gx_0'=4,'gx_1'=4,'gy_0'=4,'gy_1'=2] {'gx_1'}, use_global_device_ids=true, to_apply=%add.44 | all-reduce | flops 12 | bytes 96
  226.5 6.0 %all-reduce.77 = (f32[4]{0:T(128)S(1)}, f32[4]{0:T(128)S(1)}, f32[4]{0:T(128)S(1)}) all-reduce(f32[4]{0:T(128)S(1)} %dynamic-update-slice.18, f32[4]{0:T(128)S(1)} %dynamic-update-slice.14, f32[4]{0:T(128)S(1)} %dynamic-update-slice.22), channel_id=1, replica_groups=mesh['gx_0'=4,'gx_1'=4,'gy_0'=4,'gy_1'=2] {'gy_0'}, use_global_device_ids=true, to_apply=%add.45 | all-reduce | flops 12 | bytes 96
  238.6 7.9 %all-reduce.89 = (f32[2]{0:T(128)S(1)}, f32[2]{0:T(128)S(1)}, f32[2]{0:T(128)S(1)}) all-reduce(f32[2]{0:T(128)S(1)} %dynamic-update-slice.19, f32[2]{0:T(128)S(1)} %dynamic-update-slice.15, f32[2]{0:T(128)S(1)} %dynamic-update-slice.23), channel_id=1, replica_groups=mesh['gx_0'=4,'gx_1'=4,'gy_0'=4,'gy_1'=2] {'gy_1'}, use_global_device_ids=true, to_apply=%add.46 | all-reduce | flops 6 | bytes 48
  257.2 3.8 collective-permute-start.16
  268.4 4.5 collective-permute-done.19
  274.2 3.0 multiply_reduce_fusion.5
  278.7 9.5 %all-reduce.51 = f32[4]{0:T(128)S(1)} all-reduce(f32[4]{0:T(128)S(1)} %dynamic-update-slice.24), channel_id=1, replica_groups=mesh['gx_0'=4,'gx_1'=4,'gy_0'=4,'gy_1'=2] {'gx_0'}, use_global_device_ids=true, to_apply=%add.51 | all-reduce | flops 4 | bytes 32
  290.3 6.0 %all-reduce.52 = f32[4]{0:T(128)S(1)} all-reduce(f32[4]{0:T(128)S(1)} %dynamic-update-slice.25), channel_id=1, replica_groups=mesh['gx_0'=4,'gx_1'=4,'gy_0'=4,'gy_1'=2] {'gx_1'}, use_global_device_ids=true, to_apply=%add.52 | all-reduce | flops 4 | bytes 32
  298.4 6.8 %all-reduce.53 = f32[4]{0:T(128)S(1)} all-reduce(f32[4]{0:T(128)S(1)} %dynamic-update-slice.26), channel_id=1, replica_groups=mesh['gx_0'=4,'gx_1'=4,'gy_0'=4,'gy_1'=2] {'gy_0'}, use_global_device_ids=true, to_apply=%add.53 | all-reduce | flops 4 | bytes 32
  307.2 7.0 %all-reduce.54 = f32[2]{0:T(128)S(1)} all-reduce(f32[2]{0:T(128)S(1)} %dynamic-update-slice.27), channel_id=1, replica_groups=mesh['gx_0'=4,'gx_1'=4,'gy_0'=4,'gy_1'=2] {'gy_1'}, use_global_device_ids=true, to_apply=%add.54 | all-reduce | flops 2 | bytes 16
  318.2 3.6 collective-permute-start.20
  329.9 4.6 collective-permute-done.23
  334.5 3.3 fusion.7
  337.8 2.9 multiply_reduce_fusion.4
  343.4 9.2 %all-reduce.84 = (f32[4]{0:T(128)S(1)}, f32[4]{0:T(128)S(1)}) all-reduce(f32[4]{0:T(128)S(1)} %dynamic-update-slice.32, f32[4]{0:T(128)S(1)} %dynamic-update-slice.28), channel_id=1, replica_groups=mesh['gx_0'=4,'gx_1'=4,'gy_0'=4,'gy_1'=2] {'gx_0'}, use_global_device_ids=true, to_apply=%add.59 | all-reduce | flops 8 | bytes 64
  357.2 6.0 %all-reduce.80 = (f32[4]{0:T(128)S(1)}, f32[4]{0:T(128)S(1)}) all-reduce(f32[4]{0:T(128)S(1)} %dynamic-update-slice.33, f32[4]{0:T(128)S(1)} %dynamic-update-slice.29), channel_id=1, replica_groups=mesh['gx_0'=4,'gx_1'=4,'gy_0'=4,'gy_1'=2] {'gx_1'}, use_global_device_ids=true, to_apply=%add.60 | all-reduce | flops 8 | bytes 64
  367.5 6.0 %all-reduce.76 = (f32[4]{0:T(128)S(1)}, f32[4]{0:T(128)S(1)}) all-reduce(f32[4]{0:T(128)S(1)} %dynamic-update-slice.34, f32[4]{0:T(128)S(1)} %dynamic-update-slice.30), channel_id=1, replica_groups=mesh['gx_0'=4,'gx_1'=4,'gy_0'=4,'gy_1'=2] {'gy_0'}, use_global_device_ids=true, to_apply=%add.61 | all-reduce | flops 8 | bytes 64
  377.6 7.7 %all-reduce.88 = (f32[2]{0:T(128)S(1)}, f32[2]{0:T(128)S(1)}) all-reduce(f32[2]{0:T(128)S(1)} %dynamic-update-slice.35, f32[2]{0:T(128)S(1)} %dynamic-update-slice.31), channel_id=1, replica_groups=mesh['gx_0'=4,'gx_1'=4,'gy_0'=4,'gy_1'=2] {'gy_1'}, use_global_device_ids=true, to_apply=%add.62 | all-reduce | flops 4 | bytes 32
  392.9 3.6 collective-permute-start.24
  403.4 3.2 fusion.33
  406.6 3.0 collective-permute-done.27
  411.7 3.0 multiply_reduce_fusion
  418.8 9.5 %all-reduce.83 = (f32[4]{0:T(128)S(1)}, f32[4]{0:T(128)S(1)}, f32[4]{0:T(128)S(1)}) all-reduce(f32[4]{0:T(128)S(1)} %dynamic-update-slice.40, f32[4]{0:T(128)S(1)} %dynamic-update-slice.36, f32[4]{0:T(128)S(1)} %dynamic-update-slice.44), channel_id=1, replica_groups=mesh['gx_0'=4,'gx_1'=4,'gy_0'=4,'gy_1'=2] {'gx_0'}, use_global_device_ids=true, to_apply=%add.67 | all-reduce | flops 12 | bytes 96
  434.5 6.0 %all-reduce.79 = (f32[4]{0:T(128)S(1)}, f32[4]{0:T(128)S(1)}, f32[4]{0:T(128)S(1)}) all-reduce(f32[4]{0:T(128)S(1)} %dynamic-update-slice.41, f32[4]{0:T(128)S(1)} %dynamic-update-slice.37, f32[4]{0:T(128)S(1)} %dynamic-update-slice.45), channel_id=1, replica_groups=mesh['gx_0'=4,'gx_1'=4,'gy_0'=4,'gy_1'=2] {'gx_1'}, use_global_device_ids=true, to_apply=%add.68 | all-reduce | flops 12 | bytes 96
  447.3 6.8 %all-reduce.75 = (f32[4]{0:T(128)S(1)}, f32[4]{0:T(128)S(1)}, f32[4]{0:T(128)S(1)}) all-reduce(f32[4]{0:T(128)S(1)} %dynamic-update-slice.42, f32[4]{0:T(128)S(1)} %dynamic-update-slice.38, f32[4]{0:T(128)S(1)} %dynamic-update-slice.46), channel_id=1, replica_groups=mesh['gx_0'=4,'gx_1'=4,'gy_0'=4,'gy_1'=2] {'gy_0'}, use_global_device_ids=true, to_apply=%add.69 | all-reduce | flops 12 | bytes 96
  459.9 7.1 %all-reduce.87 = (f32[2]{0:T(128)S(1)}, f32[2]{0:T(128)S(1)}, f32[2]{0:T(128)S(1)}) all-reduce(f32[2]{0:T(128)S(1)} %dynamic-update-slice.43, f32[2]{0:T(128)S(1)} %dynamic-update-slice.39, f32[2]{0:T(128)S(1)} %dynamic-update-slice.47), channel_id=1, replica_groups=mesh['gx_0'=4,'gx_1'=4,'gy_0'=4,'gy_1'=2] {'gy_1'}, use_global_device_ids=true, to_apply=%add.70 | all-reduce | flops 6 | bytes 48
  474.7 4.4 multiply_subtract_fusion
  (332 shorter events, 187.9 us)
Async XLA Ops:
  0.6 8.2 %copy-start.1 = (f32[10,64,512]{2,1,0:T(8,128)S(1)}, f32[10,64,512]{2,1,0:T(8,128)}, u32[]{:S(2)}) copy-start(f32[10,64,512]{2,1,0:T(8,128)} %param.8) | copy-start | bytes 3932164
  1.7 14.1 %copy-start = (f32[10,64,512]{2,1,0:T(8,128)S(1)}, f32[10,64,512]{2,1,0:T(8,128)}, u32[]{:S(2)}) copy-start(f32[10,64,512]{2,1,0:T(8,128)} %param.6) | copy-start | bytes 3932164
  3.4 32.2 %collective-permute-start = (f32[11,1,512]{2,1,0:T(1,128)}, f32[11,1,512]{2,1,0:T(1,128)S(1)}, u32[]{:S(2)}, u32[]{:S(2)}) collective-permute-start(f32[11,1,512]{2,1,0:T(1,128)} %get-tuple-element.72), channel_id=1, source_target_pairs={{0,8},{8,16},{16,24},{24,32},{32,40},{40,48},{48,56},{56,64},{64,7... | collective-permute-start | bytes 67592 | tf_op jit(solution)/shard_map/ppermute | solution.py:24
  7.4 11.3 %copy-start.44 = (s32[64,512]{1,0:T(8,128)S(1)}, s32[64,512]{1,0:T(8,128)}, u32[]{:S(2)}) copy-start(s32[64,512]{1,0:T(8,128)} %param.11) | copy-start | bytes 393220
  7.4 28.3 %collective-permute-start.1 = (f32[11,1,512]{2,1,0:T(1,128)S(1)}, f32[11,1,512]{2,1,0:T(1,128)S(1)}, u32[]{:S(2)}, u32[]{:S(2)}) collective-permute-start(f32[11,1,512]{2,1,0:T(1,128)S(1)} %get-tuple-element.73), channel_id=1, source_target_pairs={{8,0},{16,8},{24,16},{32,24},{40,32},{48,40},{56,48},{64,56},{72,6... | collective-permute-start | bytes 67592 | tf_op jit(solution)/shard_map/ppermute | solution.py:25
  9.8 10.6 %collective-permute-start.2 = (f32[11,64,1]{2,1,0:T(8,128)}, f32[11,64,1]{2,1,0:T(8,128)}, u32[]{:S(2)}, u32[]{:S(2)}) collective-permute-start(f32[11,64,1]{2,1,0:T(8,128)} %get-tuple-element.74), channel_id=1, source_target_pairs={{0,1},{1,2},{2,3},{3,4},{4,5},{5,6},{6,7},{8,9},{9,10},{10,11},{11... | collective-permute-start | bytes 8456 | tf_op jit(solution)/shard_map/ppermute | solution.py:24
  13.8 12.5 %collective-permute-start.3 = (f32[11,64,1]{2,1,0:T(8,128)}, f32[11,64,1]{2,1,0:T(8,128)}, u32[]{:S(2)}, u32[]{:S(2)}) collective-permute-start(f32[11,64,1]{2,1,0:T(8,128)} %get-tuple-element.75), channel_id=1, source_target_pairs={{1,0},{2,1},{3,2},{4,3},{5,4},{6,5},{7,6},{9,8},{10,9},{11,10},{12... | collective-permute-start | bytes 8456 | tf_op jit(solution)/shard_map/ppermute | solution.py:25
  16.4 15.7 %collective-permute-start.5 = (f32[10,1,512]{2,1,0:T(1,128)}, f32[10,1,512]{2,1,0:T(1,128)S(1)}, u32[]{:S(2)}, u32[]{:S(2)}) collective-permute-start(f32[10,1,512]{2,1,0:T(1,128)} %get-tuple-element.99), channel_id=1, source_target_pairs={{8,0},{16,8},{24,16},{32,24},{40,32},{48,40},{56,48},{64,56},{72,6... | collective-permute-start | bytes 61448 | tf_op jit(solution)/shard_map/ppermute | solution.py:25
  20.4 18.1 %collective-permute-start.4 = (f32[10,1,512]{2,1,0:T(1,128)S(1)}, f32[10,1,512]{2,1,0:T(1,128)S(1)}, u32[]{:S(2)}, u32[]{:S(2)}) collective-permute-start(f32[10,1,512]{2,1,0:T(1,128)S(1)} %get-tuple-element.98), channel_id=1, source_target_pairs={{0,8},{8,16},{16,24},{24,32},{32,40},{40,48},{48,56},{56,64},{64,7... | collective-permute-start | bytes 61448 | tf_op jit(solution)/shard_map/ppermute | solution.py:24
  26.3 10.2 %copy-start.35 = (f32[11,66,1]{2,1,0:T(8,128)}, f32[11,66,1]{2,1,0:T(8,128)S(1)}, u32[]{:S(2)}) copy-start(f32[11,66,1]{2,1,0:T(8,128)S(1)} %pad.57) | copy-start | bytes 8716
  26.4 13.4 %collective-permute-start.6 = (f32[10,64,1]{2,1,0:T(8,128)}, f32[10,64,1]{2,1,0:T(8,128)}, u32[]{:S(2)}, u32[]{:S(2)}) collective-permute-start(f32[10,64,1]{2,1,0:T(8,128)} %get-tuple-element.96), channel_id=1, source_target_pairs={{0,1},{1,2},{2,3},{3,4},{4,5},{5,6},{6,7},{8,9},{9,10},{10,11},{11... | collective-permute-start | bytes 7688 | tf_op jit(solution)/shard_map/ppermute | solution.py:24
  32.1 8.7 %collective-permute-start.7 = (f32[10,64,1]{2,1,0:T(8,128)}, f32[10,64,1]{2,1,0:T(8,128)}, u32[]{:S(2)}, u32[]{:S(2)}) collective-permute-start(f32[10,64,1]{2,1,0:T(8,128)} %get-tuple-element.97), channel_id=1, source_target_pairs={{1,0},{2,1},{3,2},{4,3},{5,4},{6,5},{7,6},{9,8},{10,9},{11,10},{12... | collective-permute-start | bytes 7688 | tf_op jit(solution)/shard_map/ppermute | solution.py:25
  46.0 19.4 %copy-start.46 = (u32[128]{0:T(128)S(1)}, u32[128]{0:T(128)}, u32[]{:S(2)}) copy-start(u32[128]{0:T(128)} %constant.89) | copy-start | bytes 1540
  46.0 28.6 %copy-start.45 = (u32[128]{0:T(128)S(1)}, u32[128]{0:T(128)}, u32[]{:S(2)}) copy-start(u32[128]{0:T(128)} %constant.94) | copy-start | bytes 1540
  94.6 10.9 %copy-start.17 = (f32[9,64,512]{2,1,0:T(8,128)S(1)}, f32[9,64,512]{2,1,0:T(8,128)}, u32[]{:S(2)}) copy-start(f32[9,64,512]{2,1,0:T(8,128)} %get-tuple-element.69) | copy-start | bytes 3538948
  96.4 10.0 %collective-permute-start.8 = (f32[10,1,512]{2,1,0:T(1,128)S(1)}, f32[10,1,512]{2,1,0:T(1,128)S(1)}, u32[]{:S(2)}, u32[]{:S(2)}) collective-permute-start(f32[10,1,512]{2,1,0:T(1,128)S(1)} %get-tuple-element.94), channel_id=1, source_target_pairs={{0,8},{8,16},{16,24},{24,32},{32,40},{40,48},{48,56},{56,64},{64,7... | collective-permute-start | bytes 61448 | tf_op jit(solution)/shard_map/ppermute | solution.py:24
  99.4 7.0 %collective-permute-start.9 = (f32[10,1,512]{2,1,0:T(1,128)S(1)}, f32[10,1,512]{2,1,0:T(1,128)S(1)}, u32[]{:S(2)}, u32[]{:S(2)}) collective-permute-start(f32[10,1,512]{2,1,0:T(1,128)S(1)} %get-tuple-element.95), channel_id=1, source_target_pairs={{8,0},{16,8},{24,16},{32,24},{40,32},{48,40},{56,48},{64,56},{72,6... | collective-permute-start | bytes 61448 | tf_op jit(solution)/shard_map/ppermute | solution.py:25
  100.7 9.2 %collective-permute-start.10 = (f32[10,64,1]{2,1,0:T(8,128)S(1)}, f32[10,64,1]{2,1,0:T(8,128)S(1)}, u32[]{:S(2)}, u32[]{:S(2)}) collective-permute-start(f32[10,64,1]{2,1,0:T(8,128)S(1)} %get-tuple-element.92), channel_id=1, source_target_pairs={{0,1},{1,2},{2,3},{3,4},{4,5},{5,6},{6,7},{8,9},{9,10},{10,11},{11... | collective-permute-start | bytes 7688 | tf_op jit(solution)/shard_map/ppermute | solution.py:24
  102.7 8.4 %collective-permute-start.11 = (f32[10,64,1]{2,1,0:T(8,128)S(1)}, f32[10,64,1]{2,1,0:T(8,128)S(1)}, u32[]{:S(2)}, u32[]{:S(2)}) collective-permute-start(f32[10,64,1]{2,1,0:T(8,128)S(1)} %get-tuple-element.93), channel_id=1, source_target_pairs={{1,0},{2,1},{3,2},{4,3},{5,4},{6,5},{7,6},{9,8},{10,9},{11,10},{12... | collective-permute-start | bytes 7688 | tf_op jit(solution)/shard_map/ppermute | solution.py:25
  170.4 19.6 %copy-start.6 = (f32[10,64,512]{2,1,0:T(8,128)}, f32[10,64,512]{2,1,0:T(8,128)S(1)}, u32[]{:S(2)}) copy-start(f32[10,64,512]{2,1,0:T(8,128)S(1)} %subtract_divide_fusion.1) | copy-start | bytes 3932164
  172.3 10.4 %collective-permute-start.12 = (f32[10,1,512]{2,1,0:T(1,128)S(1)}, f32[10,1,512]{2,1,0:T(1,128)S(1)}, u32[]{:S(2)}, u32[]{:S(2)}) collective-permute-start(f32[10,1,512]{2,1,0:T(1,128)S(1)} %get-tuple-element.90), channel_id=1, source_target_pairs={{0,8},{8,16},{16,24},{24,32},{32,40},{40,48},{48,56},{56,64},{64,7... | collective-permute-start | bytes 61448 | tf_op jit(solution)/shard_map/ppermute | solution.py:24
  175.9 6.8 %collective-permute-start.13 = (f32[10,1,512]{2,1,0:T(1,128)S(1)}, f32[10,1,512]{2,1,0:T(1,128)S(1)}, u32[]{:S(2)}, u32[]{:S(2)}) collective-permute-start(f32[10,1,512]{2,1,0:T(1,128)S(1)} %get-tuple-element.91), channel_id=1, source_target_pairs={{8,0},{16,8},{24,16},{32,24},{40,32},{48,40},{56,48},{64,56},{72,6... | collective-permute-start | bytes 61448 | tf_op jit(solution)/shard_map/ppermute | solution.py:25
  178.1 7.1 %collective-permute-start.14 = (f32[10,64,1]{2,1,0:T(8,128)}, f32[10,64,1]{2,1,0:T(8,128)S(1)}, u32[]{:S(2)}, u32[]{:S(2)}) collective-permute-start(f32[10,64,1]{2,1,0:T(8,128)} %get-tuple-element.88), channel_id=1, source_target_pairs={{0,1},{1,2},{2,3},{3,4},{4,5},{5,6},{6,7},{8,9},{9,10},{10,11},{11... | collective-permute-start | bytes 7688 | tf_op jit(solution)/shard_map/ppermute | solution.py:24
  180.7 8.6 %collective-permute-start.15 = (f32[10,64,1]{2,1,0:T(8,128)}, f32[10,64,1]{2,1,0:T(8,128)S(1)}, u32[]{:S(2)}, u32[]{:S(2)}) collective-permute-start(f32[10,64,1]{2,1,0:T(8,128)} %get-tuple-element.89), channel_id=1, source_target_pairs={{1,0},{2,1},{3,2},{4,3},{5,4},{6,5},{7,6},{9,8},{10,9},{11,10},{12... | collective-permute-start | bytes 7688 | tf_op jit(solution)/shard_map/ppermute | solution.py:25
  257.2 9.8 %copy-start.2 = (f32[10,64,512]{2,1,0:T(8,128)S(1)}, f32[10,64,512]{2,1,0:T(8,128)}, u32[]{:S(2)}) copy-start(f32[10,64,512]{2,1,0:T(8,128)} %param.8) | copy-start | bytes 3932164
  257.2 9.8 %collective-permute-start.16 = (f32[10,1,512]{2,1,0:T(1,128)S(1)}, f32[10,1,512]{2,1,0:T(1,128)S(1)}, u32[]{:S(2)}, u32[]{:S(2)}) collective-permute-start(f32[10,1,512]{2,1,0:T(1,128)S(1)} %get-tuple-element.86), channel_id=1, source_target_pairs={{0,8},{8,16},{16,24},{24,32},{32,40},{40,48},{48,56},{56,64},{64,7... | collective-permute-start | bytes 61448 | tf_op jit(solution)/shard_map/ppermute | solution.py:24
  261.0 6.0 %collective-permute-start.17 = (f32[10,1,512]{2,1,0:T(1,128)S(1)}, f32[10,1,512]{2,1,0:T(1,128)S(1)}, u32[]{:S(2)}, u32[]{:S(2)}) collective-permute-start(f32[10,1,512]{2,1,0:T(1,128)S(1)} %get-tuple-element.87), channel_id=1, source_target_pairs={{8,0},{16,8},{24,16},{32,24},{40,32},{48,40},{56,48},{64,56},{72,6... | collective-permute-start | bytes 61448 | tf_op jit(solution)/shard_map/ppermute | solution.py:25
  262.5 5.9 %collective-permute-start.18 = (f32[10,64,1]{2,1,0:T(8,128)S(1)}, f32[10,64,1]{2,1,0:T(8,128)S(1)}, u32[]{:S(2)}, u32[]{:S(2)}) collective-permute-start(f32[10,64,1]{2,1,0:T(8,128)S(1)} %get-tuple-element.84), channel_id=1, source_target_pairs={{0,1},{1,2},{2,3},{3,4},{4,5},{5,6},{6,7},{8,9},{9,10},{10,11},{11... | collective-permute-start | bytes 7688 | tf_op jit(solution)/shard_map/ppermute | solution.py:24
  264.4 8.5 %copy-start.23 = (f32[10,64,513]{2,1,0:T(8,128)S(1)}, f32[10,64,513]{2,1,0:T(8,128)}, u32[]{:S(2)}) copy-start(f32[10,64,513]{2,1,0:T(8,128)} %get-tuple-element.71) | copy-start | bytes 3939844
  264.4 8.5 %collective-permute-start.19 = (f32[10,64,1]{2,1,0:T(8,128)S(1)}, f32[10,64,1]{2,1,0:T(8,128)S(1)}, u32[]{:S(2)}, u32[]{:S(2)}) collective-permute-start(f32[10,64,1]{2,1,0:T(8,128)S(1)} %get-tuple-element.85), channel_id=1, source_target_pairs={{1,0},{2,1},{3,2},{4,3},{5,4},{6,5},{7,6},{9,8},{10,9},{11,10},{12... | collective-permute-start | bytes 7688 | tf_op jit(solution)/shard_map/ppermute | solution.py:25
  318.2 9.8 %collective-permute-start.20 = (f32[10,1,512]{2,1,0:T(1,128)S(1)}, f32[10,1,512]{2,1,0:T(1,128)S(1)}, u32[]{:S(2)}, u32[]{:S(2)}) collective-permute-start(f32[10,1,512]{2,1,0:T(1,128)S(1)} %get-tuple-element.82), channel_id=1, source_target_pairs={{0,8},{8,16},{16,24},{24,32},{32,40},{40,48},{48,56},{56,64},{64,7... | collective-permute-start | bytes 61448 | tf_op jit(solution)/shard_map/ppermute | solution.py:24
  321.8 6.2 %collective-permute-start.21 = (f32[10,1,512]{2,1,0:T(1,128)S(1)}, f32[10,1,512]{2,1,0:T(1,128)S(1)}, u32[]{:S(2)}, u32[]{:S(2)}) collective-permute-start(f32[10,1,512]{2,1,0:T(1,128)S(1)} %get-tuple-element.83), channel_id=1, source_target_pairs={{8,0},{16,8},{24,16},{32,24},{40,32},{48,40},{56,48},{64,56},{72,6... | collective-permute-start | bytes 61448 | tf_op jit(solution)/shard_map/ppermute | solution.py:25
  323.3 6.6 %collective-permute-start.22 = (f32[10,64,1]{2,1,0:T(8,128)S(1)}, f32[10,64,1]{2,1,0:T(8,128)S(1)}, u32[]{:S(2)}, u32[]{:S(2)}) collective-permute-start(f32[10,64,1]{2,1,0:T(8,128)S(1)} %get-tuple-element.80), channel_id=1, source_target_pairs={{0,1},{1,2},{2,3},{3,4},{4,5},{5,6},{6,7},{8,9},{9,10},{10,11},{11... | collective-permute-start | bytes 7688 | tf_op jit(solution)/shard_map/ppermute | solution.py:24
  325.9 8.6 %copy-start.24 = (f32[10,64,513]{2,1,0:T(8,128)S(1)}, f32[10,64,513]{2,1,0:T(8,128)}, u32[]{:S(2)}) copy-start(f32[10,64,513]{2,1,0:T(8,128)} %get-tuple-element.71) | copy-start | bytes 3939844
  325.9 8.6 %copy-start.39 = (f32[10,64,1]{2,1,0:T(8,128)S(1)}, f32[10,64,1]{2,1,0:T(8,128)}, u32[]{:S(2)}) copy-start(f32[10,64,1]{2,1,0:T(8,128)} %copy-done.38) | copy-start | bytes 7684
  325.9 8.5 %copy-start.41 = (f32[10,64,1]{2,1,0:T(8,128)S(1)}, f32[10,64,1]{2,1,0:T(8,128)}, u32[]{:S(2)}) copy-start(f32[10,64,1]{2,1,0:T(8,128)} %copy-done.40) | copy-start | bytes 7684
  325.9 8.5 %collective-permute-start.23 = (f32[10,64,1]{2,1,0:T(8,128)S(1)}, f32[10,64,1]{2,1,0:T(8,128)S(1)}, u32[]{:S(2)}, u32[]{:S(2)}) collective-permute-start(f32[10,64,1]{2,1,0:T(8,128)S(1)} %get-tuple-element.81), channel_id=1, source_target_pairs={{1,0},{2,1},{3,2},{4,3},{5,4},{6,5},{7,6},{9,8},{10,9},{11,10},{12... | collective-permute-start | bytes 7688 | tf_op jit(solution)/shard_map/ppermute | solution.py:25
  329.8 7.9 %copy-start.11 = (f32[10,64,512]{2,1,0:T(8,128)S(1)}, f32[10,64,512]{2,1,0:T(8,128)}, u32[]{:S(2)}) copy-start(f32[10,64,512]{2,1,0:T(8,128)} %param.9) | copy-start | bytes 3932164
  329.8 7.9 %copy-start.15 = (f32[10,64,512]{2,1,0:T(8,128)S(1)}, f32[10,64,512]{2,1,0:T(8,128)}, u32[]{:S(2)}) copy-start(f32[10,64,512]{2,1,0:T(8,128)} %get-tuple-element.58) | copy-start | bytes 3932164
  391.0 6.9 %copy-start.3 = (f32[10,64,512]{2,1,0:T(8,128)}, f32[10,64,512]{2,1,0:T(8,128)S(1)}, u32[]{:S(2)}) copy-start(f32[10,64,512]{2,1,0:T(8,128)S(1)} %subtract_divide_fusion) | copy-start | bytes 3932164
  392.9 10.5 %collective-permute-start.24 = (f32[10,1,512]{2,1,0:T(1,128)S(1)}, f32[10,1,512]{2,1,0:T(1,128)S(1)}, u32[]{:S(2)}, u32[]{:S(2)}) collective-permute-start(f32[10,1,512]{2,1,0:T(1,128)S(1)} %get-tuple-element.78), channel_id=1, source_target_pairs={{0,8},{8,16},{16,24},{24,32},{32,40},{40,48},{48,56},{56,64},{64,7... | collective-permute-start | bytes 61448 | tf_op jit(solution)/shard_map/ppermute | solution.py:24
  396.5 6.9 %collective-permute-start.25 = (f32[10,1,512]{2,1,0:T(1,128)S(1)}, f32[10,1,512]{2,1,0:T(1,128)S(1)}, u32[]{:S(2)}, u32[]{:S(2)}) collective-permute-start(f32[10,1,512]{2,1,0:T(1,128)S(1)} %get-tuple-element.79), channel_id=1, source_target_pairs={{8,0},{16,8},{24,16},{32,24},{40,32},{48,40},{56,48},{64,56},{72,6... | collective-permute-start | bytes 61448 | tf_op jit(solution)/shard_map/ppermute | solution.py:25
  398.8 7.8 %collective-permute-start.26 = (f32[10,64,1]{2,1,0:T(8,128)}, f32[10,64,1]{2,1,0:T(8,128)S(1)}, u32[]{:S(2)}, u32[]{:S(2)}) collective-permute-start(f32[10,64,1]{2,1,0:T(8,128)} %get-tuple-element.76), channel_id=1, source_target_pairs={{0,1},{1,2},{2,3},{3,4},{4,5},{5,6},{6,7},{8,9},{9,10},{10,11},{11... | collective-permute-start | bytes 7688 | tf_op jit(solution)/shard_map/ppermute | solution.py:24
  400.7 8.9 %copy-start.4 = (f32[10,64,512]{2,1,0:T(8,128)S(1)}, f32[10,64,512]{2,1,0:T(8,128)}, u32[]{:S(2)}) copy-start(f32[10,64,512]{2,1,0:T(8,128)} %copy-done.3) | copy-start | bytes 3932164
  400.7 8.9 %copy-start.27 = (f32[10,64,513]{2,1,0:T(8,128)S(1)}, f32[10,64,513]{2,1,0:T(8,128)}, u32[]{:S(2)}) copy-start(f32[10,64,513]{2,1,0:T(8,128)} %get-tuple-element.55) | copy-start | bytes 3939844
  400.7 8.9 %copy-start.28 = (f32[10,64,513]{2,1,0:T(8,128)S(1)}, f32[10,64,513]{2,1,0:T(8,128)}, u32[]{:S(2)}) copy-start(f32[10,64,513]{2,1,0:T(8,128)} %get-tuple-element.56) | copy-start | bytes 3939844
  400.7 8.9 %collective-permute-start.27 = (f32[10,64,1]{2,1,0:T(8,128)}, f32[10,64,1]{2,1,0:T(8,128)S(1)}, u32[]{:S(2)}, u32[]{:S(2)}) collective-permute-start(f32[10,64,1]{2,1,0:T(8,128)} %get-tuple-element.77), channel_id=1, source_target_pairs={{1,0},{2,1},{3,2},{4,3},{5,4},{6,5},{7,6},{9,8},{10,9},{11,10},{12... | collective-permute-start | bytes 7688 | tf_op jit(solution)/shard_map/ppermute | solution.py:25
  411.7 63.0 %copy-start.5 = (f32[10,64,512]{2,1,0:T(8,128)S(1)}, f32[10,64,512]{2,1,0:T(8,128)}, u32[]{:S(2)}) copy-start(f32[10,64,512]{2,1,0:T(8,128)} %copy-done.3) | copy-start | bytes 3932164
  (29 other events, 100.3 us)
